TPU v7x, 32 devices: a whole 2x2x4 slice. The times are simulated.
32 devices in a mesh: section: 8 (over z, core), mp: 4 (over y, x).
Axes of the slice: x: 2, y: 2, z: 4, core: 2. Of those that a mesh axis runs over, the one named last changes fastest.
Arguments:
- arrive_rows: bfloat16 [8, 64, 1024], P('section'), may hold values from -50 to 50
- arrive_grads: bfloat16 [8, 64, 1024], P('section'), may hold values from -6 to 6
- feed_rows: bfloat16 [4, 64, 1024], replicated, may hold values from -50 to 50
- feed_grads: bfloat16 [4, 64, 1024], replicated, may hold values from -6 to 6
- stashed_rows: bfloat16 [8, 5, 64, 1024], P('section'), may hold values from -50 to 50
- slot_order: int32 [8, 5], P('section'), may hold values from 0 to 4, each once within a row
- enter_weight: bfloat16 [8, 1024, 4096], P('section', None, 'mp'), may hold values from -0.1875 to 0.1875
- leave_weight: bfloat16 [8, 4096, 1024], P('section', 'mp'), may hold values from -0.09375 to 0.09375
- norm_gain: bfloat16 [8, 1024], P('section'), may hold values from 0.099609375 to 1.8984375
Outputs:
- depart_rows: bfloat16 [8, 64, 1024], P('section')
- depart_grads: bfloat16 [8, 64, 1024], P('section')
- enter_update: bfloat16 [8, 1024, 4096], P('section', None, 'mp')
- leave_update: bfloat16 [8, 4096, 1024], P('section', 'mp')
- gain_update: float32 [8, 1024], P('section')
Inputs may be any that keep to these rules, and one draw needn't show every extreme that they name: `slot_order`: each section's row is a permutation of 0 to 4.
All inputs are finite; a program needn't handle non-finite values.
Results may differ from a plain program's by a relative error of at most 0.025.
Values may be sent and summed in bfloat16 or wider, within the bound.
A program may use at most 128 MiB of HBM per device.

v0:
```python
import jax
import jax.numpy as jnp
from jax import lax
from jax.sharding import PartitionSpec as P

D = 1024


epsilon = 1e-06


def shifted(block, axis, distance):
    devices = range(lax.axis_size(axis))
    route = [(i - distance, i) for i in devices if i - distance in devices]
    return lax.ppermute(block, axis, route)


def against_rows(left, right):
    return lax.dot_general(
        left, right, (((1,), (1,)), ((), ())), preferred_element_type=jnp.float32
    )


def across_rows(left, right):
    return lax.dot_general(
        left, right, (((0,), (0,)), ((), ())), preferred_element_type=jnp.float32
    )


def pick_slot(values, slot_index):
    return lax.dynamic_index_in_dim(values, slot_index, 0, keepdims=False)


def local(
    arrive_rows,
    arrive_grads,
    feed_rows,
    feed_grads,
    stashed_rows,
    slot_order,
    enter_weight,
    leave_weight,
    norm_gain,
):
    section_count = lax.axis_size("section")
    position = lax.axis_index("section")
    first_section = position == 0
    last_section = position == section_count - 1
    weight_in = enter_weight[0]
    weight_out = leave_weight[0]
    gain_row = norm_gain[0].astype(jnp.float32)
    stashed = stashed_rows[0]
    plan = slot_order[0]
    step_count = stashed.shape[0]

    def normalize(rows_in):
        wide = rows_in.astype(jnp.float32)
        scaled = (wide * gain_row).astype(jnp.bfloat16)
        inverse = lax.rsqrt(jnp.sum(wide * wide, axis=1) / D + epsilon)
        projected = jnp.dot(scaled, weight_in, preferred_element_type=jnp.float32)
        return (wide, scaled, inverse, projected)

    inputs_now = arrive_rows[0]
    grads_now = arrive_grads[0]
    gain_total = jnp.zeros_like(gain_row)
    enter_total = jnp.zeros(weight_in.shape, jnp.float32)
    leave_total = jnp.zeros(weight_out.shape, jnp.float32)
    outputs = inputs_now
    input_grad = grads_now
    for step in range(step_count):
        wide, scaled, inverse, projected = normalize(inputs_now)
        fresh_hidden = jax.nn.gelu(inverse[:, None] * projected).astype(jnp.bfloat16)
        branch_local = jnp.dot(fresh_hidden, weight_out, preferred_element_type=jnp.float32)
        branch = lax.psum(branch_local.astype(jnp.bfloat16), "mp").astype(jnp.float32)
        outputs = (wide + branch).astype(jnp.bfloat16)
        slot_index = plan[step]
        slot_rows = pick_slot(stashed, slot_index)
        slot_wide, slot_scaled, slot_inverse, slot_proj = normalize(slot_rows)
        slot_preact = slot_inverse[:, None] * slot_proj
        hidden_wide, slope_fn = jax.vjp(jax.nn.gelu, slot_preact)
        slot_hidden = hidden_wide.astype(jnp.bfloat16)
        hidden_grad = against_rows(grads_now, weight_out)
        pre_grad = slope_fn(hidden_grad)[0]
        scaled_grad = (slot_inverse[:, None] * pre_grad).astype(jnp.bfloat16)
        inverse_local = jnp.sum(pre_grad * slot_proj, axis=1)
        input_local = against_rows(scaled_grad, weight_in)
        input_part, inverse_grad = (
            lax.psum(input_local.astype(jnp.bfloat16), "mp").astype(jnp.float32),
            lax.psum(inverse_local.astype(jnp.bfloat16), "mp").astype(jnp.float32),
        )
        norm_factor = -inverse_grad * slot_inverse * slot_inverse * slot_inverse / D
        input_grad = (
            grads_now.astype(jnp.float32) + input_part * gain_row + norm_factor[:, None] * slot_wide
        ).astype(jnp.bfloat16)
        gain_total = gain_total + jnp.sum(input_part * slot_wide, axis=0)
        leave_total = leave_total + across_rows(slot_hidden, grads_now)
        enter_total = enter_total + across_rows(slot_scaled, scaled_grad)
        if step + 1 < step_count:
            moved_rows = shifted(outputs, "section", 1)
            inputs_now = jnp.where(first_section, feed_rows[step], moved_rows)
            returned = shifted(input_grad, "section", -1)
            grads_now = jnp.where(last_section, feed_grads[step], returned)
    return (
        outputs[None],
        input_grad[None],
        enter_total.astype(jnp.bfloat16)[None],
        leave_total.astype(jnp.bfloat16)[None],
        gain_total[None],
    )


def solution(mesh):
    placed = (
        P("section", None, None),
        P("section", None, None),
        P(),
        P(),
        P("section", None, None, None),
        P("section", None),
        P("section", None, "mp"),
        P("section", "mp", None),
        P("section", None),
    )
    return jax.shard_map(
        local,
        mesh=mesh,
        in_specs=placed,
        out_specs=(
            P("section", None, None),
            P("section", None, None),
            P("section", None, "mp"),
            P("section", "mp", None),
            P("section", None),
        ),
        check_vma=False,
    )
```

profile of v0, /device:TPU:0, one launch (start us, length us, event | category | flops | bytes accessed | tf_op | source)
XLA Modules:
  0.0 330.8 jit_solution(10893328931699611098)
XLA Ops:
  25.8 3.2 fusion.82
  37.4 11.5 %psum.111 = bf16[64]{0:T(256)(128)(2,1)S(1)} all-reduce(bf16[64]{0:T(256)(128)(2,1)S(1)} %copy-done.30), channel_id=1, replica_groups=mesh['section'=8,'mp'=4] {'mp'}, use_global_device_ids=true, to_apply=%region_13.14 | all-reduce | flops 64 | bytes 256 | tf_op jit(solution)/shard_map/psum | solution.py:89
  50.7 24.3 %all-reduce.19.cloned.1.call-done = (bf16[64,1024]{1,0:T(8,128)(2,1)}, bf16[64,1024]{1,0:T(8,128)(2,1)}) async-done(((bf16[64,1024]{1,0:T(8,128)(2,1)}, bf16[64,1024]{1,0:T(8,128)(2,1)}), (bf16[64,1024]{1,0:T(8,128)(2,1)}, bf16[64,1024]{1,0:T(8,128)(2,1)})) %all-reduce.19.cloned.1.call-update) | async-done | bytes 262160 | tf_op jit(solution)/shard_map/psum | solution.py:74
  78.3 3.0 collective-permute-start
  82.3 3.2 multiply_reduce_fusion.3
  91.4 3.2 fusion.85
  94.6 3.7 %fusion.306 = f32[1024,1024]{1,0:T(8,128)} fusion(f32[1024]{0:T(1024)S(1)} %bitcast.318, bf16[1,5,64,1024]{3,2,1,0:T(8,128)(2,1)S(1)} %copy-done.7, s32[]{:T(128)S(6)} %select_n.62, f32[64,1024]{1,0:T(8,128)} %copy-done.11, f32[64]{0:T(128)} %add_rsqrt_fusion.3), kind=kOutput, calls=%fused_computation.282 | convolution fusion | flops 134545408 | bytes 4591876 | tf_op jit(solution)/shard_map/dot_general | solution.py:25
  98.3 9.5 %psum.113 = bf16[64]{0:T(256)(128)(2,1)} all-reduce(bf16[64]{0:T(256)(128)(2,1)} %get-tuple-element.41), channel_id=1, replica_groups=mesh['section'=8,'mp'=4] {'mp'}, use_global_device_ids=true, to_apply=%region_17.18 | all-reduce | flops 64 | bytes 256 | tf_op jit(solution)/shard_map/psum | solution.py:89
  109.1 28.8 %all-reduce.17.cloned.1.call-done = (bf16[64,1024]{1,0:T(8,128)(2,1)}, bf16[64,1024]{1,0:T(8,128)(2,1)}) async-done(((bf16[64,1024]{1,0:T(8,128)(2,1)}, bf16[64,1024]{1,0:T(8,128)(2,1)}), (bf16[64,1024]{1,0:T(8,128)(2,1)}, bf16[64,1024]{1,0:T(8,128)(2,1)})) %all-reduce.17.cloned.1.call-update) | async-done | bytes 262160 | tf_op jit(solution)/shard_map/psum | solution.py:74
  141.2 3.2 collective-permute-start.1
  145.4 3.1 multiply_reduce_fusion.2
  154.3 3.2 fusion.88
  157.6 3.6 %fusion.302 = f32[1024,1024]{1,0:T(8,128)} fusion(f32[1024]{0:T(1024)S(1)} %bitcast.321, bf16[1,5,64,1024]{3,2,1,0:T(8,128)(2,1)S(1)} %copy-done.7, s32[]{:T(128)S(6)} %select_n.64, f32[64,1024]{1,0:T(8,128)} %copy-done.12, f32[64]{0:T(128)S(1)} %add_rsqrt_fusion.2), kind=kOutput, calls=%fused_computation.280 | convolution fusion | flops 134545408 | bytes 4592132 | tf_op jit(solution)/shard_map/dot_general | solution.py:25
  161.2 9.5 %psum.115 = bf16[64]{0:T(256)(128)(2,1)} all-reduce(bf16[64]{0:T(256)(128)(2,1)} %get-tuple-element.43), channel_id=1, replica_groups=mesh['section'=8,'mp'=4] {'mp'}, use_global_device_ids=true, to_apply=%region_21.22 | all-reduce | flops 64 | bytes 256 | tf_op jit(solution)/shard_map/psum | solution.py:89
  171.4 29.4 %all-reduce.15.cloned.1.call-done = (bf16[64,1024]{1,0:T(8,128)(2,1)}, bf16[64,1024]{1,0:T(8,128)(2,1)}) async-done(((bf16[64,1024]{1,0:T(8,128)(2,1)}, bf16[64,1024]{1,0:T(8,128)(2,1)}), (bf16[64,1024]{1,0:T(8,128)(2,1)}, bf16[64,1024]{1,0:T(8,128)(2,1)})) %all-reduce.15.cloned.1.call-update) | async-done | bytes 262160 | tf_op jit(solution)/shard_map/psum | solution.py:74
  204.1 3.0 collective-permute-start.2
  214.8 3.2 fusion.91
  220.9 9.2 %psum.117 = bf16[64]{0:T(256)(128)(2,1)S(1)} all-reduce(bf16[64]{0:T(256)(128)(2,1)} %get-tuple-element.45), channel_id=1, replica_groups=mesh['section'=8,'mp'=4] {'mp'}, use_global_device_ids=true, to_apply=%region_25.26 | all-reduce | flops 64 | bytes 256 | tf_op jit(solution)/shard_map/psum | solution.py:89
  230.0 31.3 %all-reduce.13.cloned.1.call-done = (bf16[64,1024]{1,0:T(8,128)(2,1)}, bf16[64,1024]{1,0:T(8,128)(2,1)}) async-done(((bf16[64,1024]{1,0:T(8,128)(2,1)}, bf16[64,1024]{1,0:T(8,128)(2,1)}), (bf16[64,1024]{1,0:T(8,128)(2,1)}, bf16[64,1024]{1,0:T(8,128)(2,1)})) %all-reduce.13.cloned.1.call-update) | async-done | bytes 262160 | tf_op jit(solution)/shard_map/psum | solution.py:74
  264.6 3.0 collective-permute-start.3
  273.7 3.2 fusion.94
  276.9 8.5 %fusion = bf16[1,1024,1024]{2,1,0:T(8,128)(2,1)} fusion(f32[1024,1024]{1,0:T(8,128)} %fusion.282, f32[1024,1024]{1,0:T(8,128)} %fusion.281, f32[1024,1024]{1,0:T(8,128)} %fusion.279, f32[1024,1024]{1,0:T(8,128)} %fusion.280, bf16[64,1024]{1,0:T(8,128)(2,1)S(1)} %bitcast_select_fusion.3, f32[64,1024]{1,0:T(8,128)S(1)} %fusion.23, f32[64]{0:T(128)S(1)} %add_rsqrt_fusion), kind=kOutput, calls=%fused_computation.2 | convolution fusion | flops 140115968 | bytes 19267840 | tf_op jit(solution)/shard_map/dot_general | solution.py:25
  290.9 8.9 %psum.119 = bf16[64]{0:T(256)(128)(2,1)S(1)} all-reduce(bf16[64]{0:T(256)(128)(2,1)S(1)} %get-tuple-element.47), channel_id=1, replica_groups=mesh['section'=8,'mp'=4] {'mp'}, use_global_device_ids=true, to_apply=%region_29.30 | all-reduce | flops 64 | bytes 256 | tf_op jit(solution)/shard_map/psum | solution.py:89
  299.9 20.2 %all-reduce.11.cloned.1.call-done = (bf16[64,1024]{1,0:T(8,128)(2,1)}, bf16[64,1024]{1,0:T(8,128)(2,1)}) async-done(((bf16[64,1024]{1,0:T(8,128)(2,1)}, bf16[64,1024]{1,0:T(8,128)(2,1)}), (bf16[64,1024]{1,0:T(8,128)(2,1)}, bf16[64,1024]{1,0:T(8,128)(2,1)})) %all-reduce.11.cloned.1.call-update) | async-done | bytes 262160 | tf_op jit(solution)/shard_map/psum | solution.py:74
  (142 shorter events, 73.8 us)
Async XLA Ops:
  7.2 14.1 %copy-start = (bf16[1,1024,1024]{2,1,0:T(8,128)(2,1)S(1)}, bf16[1,1024,1024]{2,1,0:T(8,128)(2,1)}, u32[]{:S(2)}) copy-start(bf16[1,1024,1024]{2,1,0:T(8,128)(2,1)} %param.15) | copy-start | bytes 6291460
  7.2 15.4 %copy-start.17 = (bf16[1,64,1024]{2,1,0:T(8,128)(2,1)S(1)}, bf16[1,64,1024]{2,1,0:T(8,128)(2,1)}, u32[]{:S(2)}) copy-start(bf16[1,64,1024]{2,1,0:T(8,128)(2,1)} %param.10) | copy-start | bytes 393220
  7.2 67.8 %all-reduce.19.cloned.1.call-start = ((), (), s32[]{:S(2)}) async-start(), calls=%async_computation.4 | async-start | bytes 524288 | tf_op jit(solution)/shard_map/psum | solution.py:74
  20.5 29.0 %copy-start.27 = (f32[64]{0:T(128)}, f32[64]{0:T(128)S(1)}, u32[]{:S(2)}) copy-start(f32[64]{0:T(128)S(1)} %get-tuple-element.12) | copy-start | bytes 772
  20.5 29.6 %copy-start.26 = (f32[64]{0:T(128)}, f32[64]{0:T(128)S(1)}, u32[]{:S(2)}) copy-start(f32[64]{0:T(128)S(1)} %get-tuple-element.11) | copy-start | bytes 772
  29.0 108.9 %all-reduce.17.cloned.1.call-start = ((), (), s32[]{:S(2)}) async-start(), calls=%async_computation.3 | async-start | bytes 524288 | tf_op jit(solution)/shard_map/psum | solution.py:74
  34.7 14.2 %copy-start.29 = (f32[64]{0:T(128)S(1)}, f32[64]{0:T(128)}, u32[]{:S(2)}) copy-start(f32[64]{0:T(128)} %copy-done.28) | copy-start | bytes 772
  34.7 15.4 %copy-start.24 = (f32[64]{0:T(128)S(1)}, f32[64]{0:T(128)}, u32[]{:S(2)}) copy-start(f32[64]{0:T(128)} %get-tuple-element.14) | copy-start | bytes 772
  34.8 15.4 %copy-start.22 = (f32[64]{0:T(128)S(1)}, f32[64]{0:T(128)}, u32[]{:S(2)}) copy-start(f32[64]{0:T(128)} %get-tuple-element.10) | copy-start | bytes 772
  37.4 37.5 %copy-start.18 = (bf16[1,64,1024]{2,1,0:T(8,128)(2,1)S(1)}, bf16[1,64,1024]{2,1,0:T(8,128)(2,1)}, u32[]{:S(2)}) copy-start(bf16[1,64,1024]{2,1,0:T(8,128)(2,1)} %param.10) | copy-start | bytes 393220
  76.0 5.3 %collective-permute-start.4 = (bf16[64,1024]{1,0:T(8,128)(2,1)S(1)}, bf16[64,1024]{1,0:T(8,128)(2,1)S(1)}, u32[]{:S(2)}, u32[]{:S(2)}) collective-permute-start(bf16[64,1024]{1,0:T(8,128)(2,1)S(1)} %fusion.121), channel_id=1, source_target_pairs={{4,0},{8,4},{12,8},{16,12},{20,16},{24,20},{28,24},{5,1},{9,5},{13... | collective-permute-start | bytes 393224 | tf_op jit(solution)/shard_map/ppermute | solution.py:15
  78.3 11.4 %collective-permute-start = (bf16[64,1024]{1,0:T(8,128)(2,1)S(1)}, bf16[64,1024]{1,0:T(8,128)(2,1)S(1)}, u32[]{:S(2)}, u32[]{:S(2)}) collective-permute-start(bf16[64,1024]{1,0:T(8,128)(2,1)S(1)} %fusion.135), channel_id=1, source_target_pairs={{0,4},{4,8},{8,12},{12,16},{16,20},{20,24},{24,28},{1,5},{5,9},{9,... | collective-permute-start | bytes 393224 | tf_op jit(solution)/shard_map/ppermute | solution.py:15
  94.6 106.2 %all-reduce.15.cloned.1.call-start = ((), (), s32[]{:S(2)}) async-start(), calls=%async_computation.2 | async-start | bytes 524288 | tf_op jit(solution)/shard_map/psum | solution.py:74
  138.9 5.5 %collective-permute-start.5 = (bf16[64,1024]{1,0:T(8,128)(2,1)S(1)}, bf16[64,1024]{1,0:T(8,128)(2,1)S(1)}, u32[]{:S(2)}, u32[]{:S(2)}) collective-permute-start(bf16[64,1024]{1,0:T(8,128)(2,1)S(1)} %fusion.124), channel_id=1, source_target_pairs={{4,0},{8,4},{12,8},{16,12},{20,16},{24,20},{28,24},{5,1},{9,5},{13... | collective-permute-start | bytes 393224 | tf_op jit(solution)/shard_map/ppermute | solution.py:15
  141.2 11.5 %collective-permute-start.1 = (bf16[64,1024]{1,0:T(8,128)(2,1)S(1)}, bf16[64,1024]{1,0:T(8,128)(2,1)S(1)}, u32[]{:S(2)}, u32[]{:S(2)}) collective-permute-start(bf16[64,1024]{1,0:T(8,128)(2,1)S(1)} %fusion.203), channel_id=1, source_target_pairs={{0,4},{4,8},{8,12},{12,16},{16,20},{20,24},{24,28},{1,5},{5,9},{9,... | collective-permute-start | bytes 393224 | tf_op jit(solution)/shard_map/ppermute | solution.py:15
  157.5 103.9 %all-reduce.13.cloned.1.call-start = ((), (), s32[]{:S(2)}) async-start(), calls=%async_computation.1 | async-start | bytes 524288 | tf_op jit(solution)/shard_map/psum | solution.py:74
  201.8 5.3 %collective-permute-start.6 = (bf16[64,1024]{1,0:T(8,128)(2,1)S(1)}, bf16[64,1024]{1,0:T(8,128)(2,1)S(1)}, u32[]{:S(2)}, u32[]{:S(2)}) collective-permute-start(bf16[64,1024]{1,0:T(8,128)(2,1)S(1)} %fusion.127), channel_id=1, source_target_pairs={{4,0},{8,4},{12,8},{16,12},{20,16},{24,20},{28,24},{5,1},{9,5},{13... | collective-permute-start | bytes 393224 | tf_op jit(solution)/shard_map/ppermute | solution.py:15
  204.1 9.7 %collective-permute-start.2 = (bf16[64,1024]{1,0:T(8,128)(2,1)S(1)}, bf16[64,1024]{1,0:T(8,128)(2,1)S(1)}, u32[]{:S(2)}, u32[]{:S(2)}) collective-permute-start(bf16[64,1024]{1,0:T(8,128)(2,1)S(1)} %fusion.220), channel_id=1, source_target_pairs={{0,4},{4,8},{8,12},{12,16},{16,20},{20,24},{24,28},{1,5},{5,9},{9,... | collective-permute-start | bytes 393224 | tf_op jit(solution)/shard_map/ppermute | solution.py:15
  218.1 12.0 %copy-start.25 = (f32[64]{0:T(128)S(1)}, f32[64]{0:T(128)}, u32[]{:S(2)}) copy-start(f32[64]{0:T(128)} %get-tuple-element.14) | copy-start | bytes 772
  218.1 102.0 %all-reduce.11.cloned.1.call-start = ((), (), s32[]{:S(2)}) async-start(), calls=%async_computation | async-start | bytes 524288 | tf_op jit(solution)/shard_map/psum | solution.py:74
  262.4 5.3 %collective-permute-start.7 = (bf16[64,1024]{1,0:T(8,128)(2,1)S(1)}, bf16[64,1024]{1,0:T(8,128)(2,1)S(1)}, u32[]{:S(2)}, u32[]{:S(2)}) collective-permute-start(bf16[64,1024]{1,0:T(8,128)(2,1)S(1)} %fusion.130), channel_id=1, source_target_pairs={{4,0},{8,4},{12,8},{16,12},{20,16},{24,20},{28,24},{5,1},{9,5},{13... | collective-permute-start | bytes 393224 | tf_op jit(solution)/shard_map/ppermute | solution.py:15
  264.6 8.0 %collective-permute-start.3 = (bf16[64,1024]{1,0:T(8,128)(2,1)S(1)}, bf16[64,1024]{1,0:T(8,128)(2,1)S(1)}, u32[]{:S(2)}, u32[]{:S(2)}) collective-permute-start(bf16[64,1024]{1,0:T(8,128)(2,1)S(1)} %fusion.237), channel_id=1, source_target_pairs={{0,4},{4,8},{8,12},{12,16},{16,20},{20,24},{24,28},{1,5},{5,9},{9,... | collective-permute-start | bytes 393224 | tf_op jit(solution)/shard_map/ppermute | solution.py:15
  288.5 33.2 %copy-start.19 = (bf16[64,1024]{1,0:T(8,128)(2,1)S(1)}, bf16[64,1024]{1,0:T(8,128)(2,1)}, u32[]{:S(2)}) copy-start(bf16[64,1024]{1,0:T(8,128)(2,1)} %get-tuple-element.24) | copy-start | bytes 393220
  288.5 33.2 %copy-start.20 = (bf16[64,1024]{1,0:T(8,128)(2,1)S(1)}, bf16[64,1024]{1,0:T(8,128)(2,1)}, u32[]{:S(2)}) copy-start(bf16[64,1024]{1,0:T(8,128)(2,1)} %get-tuple-element.22) | copy-start | bytes 393220
  (20 other events, 116.9 us)
Sparse Core Ops, SparseCore 0:
  29.1 45.8 all-reduce.18
  94.7 43.1 all-reduce.16
  157.6 43.1 all-reduce.14
  218.2 43.1 all-reduce.12
  277.0 43.0 all-reduce.10
where the time goes:
time: 332 us; the launch traced here: 331 us
  waiting for transfers between devices  134 us (40%)
  matrix products  74.5 us (22%)
  blocking collectives  48.7 us (15%)
  other arithmetic  27.2 us (8%)
  between operations  23.9 us (7%)
  starting transfers between devices  17.7 us (5%)
  local copies, waits for them, and re-layouts  4.67 us (1%)
    psum x5, waiting for transfers between devices, local(): lax.psum(branch_local.astype(jnp.bfloat16), 'mp').astype(jnp.float32)  134 us
    psum x5, blocking collectives, local(): lax.psum(inverse_local.astype(jnp.bfloat16), 'mp').astype(jnp.float32)  48.7 us
    dot_general x10, matrix products, across_rows(): lax.dot_general(left, right, (((0,), (0,)), ((), ())), preferred_element_...  34.9 us
    dot_general x10, matrix products, against_rows(): lax.dot_general(left, right, (((1,), (1,)), ((), ())), preferred_element_...  19 us
    ppermute x8, starting transfers between devices, shifted(): return lax.ppermute(block, axis, route)  17.5 us
    dot_general x5, matrix products, local(): jnp.dot(fresh_hidden, weight_out, preferred_element_type=jnp.float32)  15.9 us
  transfers between devices with their start and end apart: 13, of which 5 were waited for; matrix products, arithmetic and copies ran while one was open for 20% of the time, Pallas kernels for 0%

commit v1 on v0

v1 whole, which is shorter than its diff:
```python
import functools

import jax
import jax.numpy as jnp
from jax import lax
from jax.experimental import pallas as pl
from jax.experimental.pallas import tpu as pltpu
from jax.sharding import PartitionSpec as P

MESH = pl.DeviceIdType.MESH
F32 = jnp.float32
BF16 = jnp.bfloat16
epsilon = 1e-06
ROOT = 0.7978845608028654
CUBE = 0.044715


def dot(left, right, over_left, over_right):
    return lax.dot_general(
        left, right, (((over_left,), (over_right,)), ((), ())), preferred_element_type=F32
    )


def kernel(
    sections,
    peers,
    slot_ref,
    arrive_rows,
    arrive_grads,
    feed_rows,
    feed_grads,
    stashed,
    win,
    wout,
    gain,
    depart_rows,
    depart_grads,
    enter_out,
    leave_out,
    gain_out,
    rows_in,
    grads_in,
    part_send,
    part_recv,
    sum_send,
    own_rows,
    own_grads,
    slot_rows,
    slot_scaled,
    slot_hidden,
    slot_proj,
    slot_slope,
    slot_inverse,
    slot_update,
    grads_all,
    gain_acc,
    gain_send,
    gain_recv,
    part_ssem,
    part_rsem,
    sum_ssem,
    sum_rsem,
    gain_ssem,
    gain_rsem,
):
    sec = lax.axis_index("section")
    me = lax.axis_index("mp")
    steps, rows, width = stashed.shape
    hidden_width = win.shape[1]
    block = width // peers
    not_first = sec > 0
    not_last = sec < sections - 1

    def ahead(k):
        return lax.rem(me + k, peers)

    def behind(k):
        return lax.rem(me + peers - k, peers)

    def span(p):
        return pl.ds(pl.multiple_of(p * block, block), block)

    barrier = pltpu.get_barrier_semaphore()

    def greet(section, p):
        pl.semaphore_signal(barrier, inc=1, device_id=(section, p), device_id_type=MESH)

    for k in range(1, peers):
        greet(sec, ahead(k))

    @pl.when(not_first)
    def _():
        for k in range(peers):
            greet(sec - 1, ahead(k))

    @pl.when(not_last)
    def _():
        for k in range(peers):
            greet(sec + 1, ahead(k))

    expected = (
        peers - 1
        + peers * jnp.where(not_first, 1, 0)
        + peers * jnp.where(not_last, 1, 0)
    )

    for p in range(peers):
        cut = pl.ds(p * block, block)
        rows_in[0, p] = arrive_rows[:, cut]
        grads_in[0, p] = arrive_grads[:, cut]

    @pl.when(sec == 0)
    def _():
        for t in range(1, steps):
            for p in range(peers):
                rows_in[t, p] = feed_rows[t - 1, :, pl.ds(p * block, block)]

    @pl.when(sec == sections - 1)
    def _():
        for t in range(1, steps):
            for p in range(peers):
                grads_in[t, p] = feed_grads[t - 1, :, pl.ds(p * block, block)]

    gain_acc[...] = jnp.zeros_like(gain_acc)

    def part_copy(way, t, k):
        return pltpu.make_async_remote_copy(
            src_ref=part_send.at[way, t, k - 1],
            dst_ref=part_recv.at[way, t, k - 1],
            send_sem=part_ssem.at[way, t, k - 1],
            recv_sem=part_rsem.at[way, t, k - 1],
            device_id=(sec, ahead(k)),
            device_id_type=MESH,
        )

    def sum_copy(way, t, k, section, p):
        land = (rows_in, grads_in)[way]
        return pltpu.make_async_remote_copy(
            src_ref=sum_send.at[way, t],
            dst_ref=land.at[t + 1, me],
            send_sem=sum_ssem.at[way, t, k],
            recv_sem=sum_rsem.at[way, t, k],
            device_id=(section, p),
            device_id_type=MESH,
        )

    def sum_wait(way, t, k):
        land = (rows_in, grads_in)[way]
        pltpu.make_async_remote_copy(
            src_ref=sum_send.at[way, t],
            dst_ref=land.at[t + 1, behind(k)],
            send_sem=sum_ssem.at[way, t, k],
            recv_sem=sum_rsem.at[way, t, k],
            device_id=(sec, behind(k)),
            device_id_type=MESH,
        ).wait_recv()

    def forward(t):
        total = jnp.zeros((rows, hidden_width), F32)
        squares = jnp.zeros((rows, 1), F32)
        for k in range(peers):
            p = behind(k)

            @pl.when((t > 0) & not_first)
            def _():
                sum_wait(0, t - 1, k)

            wide = rows_in[t, p].astype(F32)
            scaled = (wide * gain[:, span(p)]).astype(BF16)
            total = total + dot(scaled, win[span(p), :], 1, 0)
            squares = squares + jnp.sum(wide * wide, axis=1, keepdims=True)
        z = lax.rsqrt(squares / width + epsilon) * total
        half = 0.5 * z
        hidden = (half + half * jnp.tanh(ROOT * (z + CUBE * (z * z * z)))).astype(BF16)

        @pl.when(t == 0)
        def _():
            pl.semaphore_wait(barrier, expected)

        for k in list(range(1, peers)) + [0]:
            part = dot(hidden, wout[:, span(ahead(k))], 1, 0)
            if k:
                part_send[0, t, k - 1] = part.astype(BF16)
                part_copy(0, t, k).start()
            else:
                own_rows[...] = part + rows_in[t, me].astype(F32)

    def prepare():
        for t in range(steps):
            slot = stashed[slot_ref[0, t]]
            slot_rows[t] = slot
            wide = slot.astype(F32)
            slot_scaled[t] = (wide * gain[...]).astype(BF16)
            slot_inverse[t] = lax.rsqrt(
                jnp.sum(wide * wide, axis=1, keepdims=True) / width + epsilon
            )
        flat = slot_scaled[...].reshape(steps * rows, width)
        slot_proj[...] = dot(flat, win[...], 1, 0).reshape(steps, rows, hidden_width)

        def shape_slot(t, carry):
            z = slot_inverse[t] * slot_proj[t]
            inner = ROOT * (z + CUBE * (z * z * z))
            bend = jnp.tanh(inner)
            half = 0.5 * z
            slot_hidden[t] = (half + half * bend).astype(BF16)
            slot_slope[t] = 0.5 * (1.0 + bend) + half * (1.0 - bend * bend) * (
                ROOT * (1.0 + (3.0 * CUBE) * (z * z))
            )
            return carry

        lax.fori_loop(0, steps, shape_slot, 0)

    def backward(t):
        total = jnp.zeros((rows, hidden_width), F32)
        for k in range(peers):
            p = behind(k)

            @pl.when((t > 0) & not_last)
            def _():
                sum_wait(1, t - 1, k)

            piece = grads_in[t, p]
            grads_all[t, :, span(p)] = piece
            total = total + dot(piece, wout[:, span(p)], 1, 1)
        pre_grad = total * slot_slope[t]
        inverse = slot_inverse[t]
        update = (inverse * pre_grad).astype(BF16)
        slot_update[t] = update
        dots = jnp.sum(pre_grad * slot_proj[t], axis=1, keepdims=True)
        factor = -dots * (inverse * inverse * inverse) / width
        for k in list(range(1, peers)) + [0]:
            p = ahead(k)
            raw = dot(update, win[span(p), :], 1, 1)
            wide = slot_rows[t, :, span(p)].astype(F32)
            gain_acc[p] += jnp.sum((raw * wide).reshape(rows // 8, 8, block), axis=0)
            part = raw * gain[:, span(p)] + factor * wide
            if k:
                part_send[1, t, k - 1] = part.astype(BF16)
                part_copy(1, t, k).start()
            else:
                own_grads[...] = part + grads_in[t, me].astype(F32)

    def reduce(way, t):
        own = (own_rows, own_grads)[way]
        land = (rows_in, grads_in)[way]
        total = own[...]
        for k in range(1, peers):
            part_copy(way, t, k).wait_recv()
            total = total + part_recv[way, t, k - 1].astype(F32)
        sum_send[way, t] = total.astype(BF16)

        @pl.when((t < steps - 1) & (not_last if way == 0 else not_first))
        def _():
            for k in range(peers):
                sum_copy(way, t, k, sec + 1 if way == 0 else sec - 1, ahead(k)).start()

        @pl.when(t == steps - 1)
        def _():
            land[steps, me] = total.astype(BF16)
            for k in range(1, peers):
                sum_copy(way, t, k, sec, ahead(k)).start()

    def gain_copy(k):
        return pltpu.make_async_remote_copy(
            src_ref=gain_send,
            dst_ref=gain_recv.at[k - 1],
            send_sem=gain_ssem.at[k - 1],
            recv_sem=gain_rsem.at[k - 1],
            device_id=(sec, ahead(k)),
            device_id_type=MESH,
        )

    chunk = min(256, hidden_width)

    def leave_grad():
        right = grads_all[...].reshape(steps * rows, width)

        def go(i, carry):
            cut = pl.ds(pl.multiple_of(i * chunk, chunk), chunk)
            left = slot_hidden[:, :, cut].reshape(steps * rows, chunk)
            leave_out[cut, :] = dot(left, right, 0, 0).astype(BF16)
            return carry

        lax.fori_loop(0, hidden_width // chunk, go, 0)

    def enter_grad():
        right = slot_update[...].reshape(steps * rows, hidden_width)
        deep = min(256, width)

        def go(i, carry):
            cut = pl.ds(pl.multiple_of(i * deep, deep), deep)
            left = slot_scaled[:, :, cut].reshape(steps * rows, deep)
            enter_out[cut, :] = dot(left, right, 0, 0).astype(BF16)
            return carry

        lax.fori_loop(0, width // deep, go, 0)

    def step(t, carry):
        forward(t)

        @pl.when(t == 0)
        def _():
            prepare()

        backward(t)

        @pl.when(t == steps - 1)
        def _():
            for p in range(peers):
                gain_send[pl.ds(p, 1), :] = jnp.sum(gain_acc[p], axis=0, keepdims=True)
            for k in range(1, peers):
                gain_copy(k).start()

        reduce(0, t)

        @pl.when(t == steps - 1)
        def _():
            leave_grad()

        reduce(1, t)
        return carry

    lax.fori_loop(0, steps, step, 0)
    enter_grad()

    gains = gain_send[...]
    for k in range(1, peers):
        gain_copy(k).wait_recv()
        gains = gains + gain_recv[k - 1]
    for p in range(peers):
        gain_out[:, pl.ds(p * block, block)] = gains[p : p + 1, :]

    for way, out in ((0, depart_rows), (1, depart_grads)):
        land = (rows_in, grads_in)[way]
        for k in range(1, peers):
            sum_wait(way, steps - 1, k)
        for p in range(peers):
            out[:, pl.ds(p * block, block)] = land[steps, p]

    for k in range(1, peers):
        gain_copy(k).wait_send()

    def drain(t, carry):
        for way in (0, 1):
            for k in range(1, peers):
                part_copy(way, t, k).wait_send()
            for k in range(peers):
                sends = not_last if way == 0 else not_first
                final = t == steps - 1
                sends = (sends & (t < steps - 1)) | final if k else sends & (t < steps - 1)

                @pl.when(sends)
                def _():
                    sum_copy(way, t, k, sec, me).wait_send()

        return carry

    lax.fori_loop(0, steps, drain, 0)


def solution(mesh):
    sections = mesh.shape["section"]
    peers = mesh.shape["mp"]

    def local(
        arrive_rows,
        arrive_grads,
        feed_rows,
        feed_grads,
        stashed_rows,
        slot_order,
        enter_weight,
        leave_weight,
        norm_gain,
    ):
        _, steps, rows, width = stashed_rows.shape
        hidden_width = enter_weight.shape[2]
        block = width // peers
        vmem = pl.BlockSpec(memory_space=pltpu.VMEM)
        dma = pltpu.SemaphoreType.DMA
        outs = pl.pallas_call(
            functools.partial(kernel, sections, peers),
            out_shape=(
                jax.ShapeDtypeStruct((rows, width), BF16),
                jax.ShapeDtypeStruct((rows, width), BF16),
                jax.ShapeDtypeStruct((width, hidden_width), BF16),
                jax.ShapeDtypeStruct((hidden_width, width), BF16),
                jax.ShapeDtypeStruct((1, width), F32),
            ),
            in_specs=[pl.BlockSpec(memory_space=pltpu.SMEM)] + [vmem] * 8,
            out_specs=[vmem] * 5,
            scratch_shapes=[
                pltpu.VMEM((steps + 1, peers, rows, block), BF16),
                pltpu.VMEM((steps + 1, peers, rows, block), BF16),
                pltpu.VMEM((2, steps, peers - 1, rows, block), BF16),
                pltpu.VMEM((2, steps, peers - 1, rows, block), BF16),
                pltpu.VMEM((2, steps, rows, block), BF16),
                pltpu.VMEM((rows, block), F32),
                pltpu.VMEM((rows, block), F32),
                pltpu.VMEM((steps, rows, width), BF16),
                pltpu.VMEM((steps, rows, width), BF16),
                pltpu.VMEM((steps, rows, hidden_width), BF16),
                pltpu.VMEM((steps, rows, hidden_width), F32),
                pltpu.VMEM((steps, rows, hidden_width), F32),
                pltpu.VMEM((steps, rows, 1), F32),
                pltpu.VMEM((steps, rows, hidden_width), BF16),
                pltpu.VMEM((steps, rows, width), BF16),
                pltpu.VMEM((peers, 8, block), F32),
                pltpu.VMEM((peers, block), F32),
                pltpu.VMEM((peers - 1, peers, block), F32),
                dma((2, steps, peers - 1)),
                dma((2, steps, peers - 1)),
                dma((2, steps, peers)),
                dma((2, steps, peers)),
                dma((peers - 1,)),
                dma((peers - 1,)),
            ],
            compiler_params=pltpu.CompilerParams(
                collective_id=0, has_side_effects=True, vmem_limit_bytes=56 * 1024 * 1024
            ),
        )(
            slot_order,
            arrive_rows[0],
            arrive_grads[0],
            feed_rows,
            feed_grads,
            stashed_rows[0],
            enter_weight[0],
            leave_weight[0],
            norm_gain.astype(F32),
        )
        rows_out, grads_out, enter_total, leave_total, gain_total = outs
        return (
            rows_out[None],
            grads_out[None],
            enter_total[None],
            leave_total[None],
            gain_total,
        )

    return jax.shard_map(
        local,
        mesh=mesh,
        in_specs=(
            P("section", None, None),
            P("section", None, None),
            P(),
            P(),
            P("section", None, None, None),
            P("section", None),
            P("section", None, "mp"),
            P("section", "mp", None),
            P("section", None),
        ),
        out_specs=(
            P("section", None, None),
            P("section", None, None),
            P("section", None, "mp"),
            P("section", "mp", None),
            P("section", None),
        ),
        check_vma=False,
    )
```

time: 332 us -> 69.4 us (0.21)
  waiting for transfers between devices: 134 us -> 0 us
  matrix products: 74.5 us -> 0 us
  Pallas kernels: 0 us -> 59 us
  blocking collectives: 48.7 us -> 0 us
  other arithmetic: 27.2 us -> 1.28 us
  between operations: 23.9 us -> 0.64 us
  starting transfers between devices: 17.7 us -> 0 us
  local copies, waits for them, and re-layouts: 4.67 us -> 8.28 us
    psum x5 -> x0, waiting for transfers between devices: 134 us -> none  [local(): lax.psum(branch_local.astype(jnp.bfloat16), 'mp').astype(jnp.float32)]
    dot_general x30 -> x0, matrix products: 74.5 us -> none  [the longest x10 34.9 us: across_rows(): lax.dot_general(left, right, (((0,), (0,)), ((), ())), preferred_element_...]
    pallas_call x0 -> x1, Pallas kernels: none -> 59 us  [local(): pl.pallas_call(functools.partial(kernel, sections, peers), out_shape=(jax...]
    psum x5 -> x0, blocking collectives: 48.7 us -> none  [local(): lax.psum(inverse_local.astype(jnp.bfloat16), 'mp').astype(jnp.float32)]
    ppermute x8 -> x0, starting transfers between devices: 17.5 us -> none  [shifted(): return lax.ppermute(block, axis, route)]
    reduce_sum x7 -> x0, other arithmetic: 8.37 us -> none  [the longest x6 6.43 us: normalize(): inverse = lax.rsqrt(jnp.sum(wide * wide, axis=1) / D + epsilon)]
    convert_element_type x8 -> x1, other arithmetic: 7.88 us -> 1.28 us  [local(): norm_gain.astype(F32)]
    unnamed x62 -> x9, local copies, waits for them, and re-layouts: 3.21 us -> 8.28 us
  transfers between devices with their start and end apart: 13 -> 0, of which waited for: 5 -> 0; matrix products, arithmetic and copies ran while one was open for 20% -> 0% of each run, Pallas kernels for 0% -> 0%
where the time goes in v1:
time: 69.4 us; the launch traced here: 69.2 us
  Pallas kernels  59 us (85%)
  local copies, waits for them, and re-layouts  8.28 us (12%)
  other arithmetic  1.28 us (2%)
    pallas_call x1, Pallas kernels, local(): pl.pallas_call(functools.partial(kernel, sections, peers), out_shape=(jax...  59 us
    unnamed x9, local copies, waits for them, and re-layouts  8.28 us

profile of v1, /device:TPU:0, one launch (start us, length us, event | category | flops | bytes accessed | tf_op | source)
XLA Modules:
  0.0 69.2 jit_solution(1700058741437645413)
XLA Ops:
  0.6 1.3 %convert_element_type.3.gain = f32[1,1024]{1,0:T(1,128)} convert(bf16[1,1024]{1,0:T(2,128)(2,1)} %param.17) | non-fusion elementwise | flops 1024 | bytes 6144 | tf_op jit(solution)/shard_map/convert_element_type | solution.py:430
  1.9 59.0 %shard_map.128 = (bf16[64,1024]{1,0:T(8,128)(2,1)}, bf16[64,1024]{1,0:T(8,128)(2,1)}, bf16[1024,1024]{1,0:T(8,128)(2,1)}, bf16[1024,1024]{1,0:T(8,128)(2,1)}, f32[1,1024]{1,0:T(1,128)}) custom-call(s32[1,5]{1,0:T(1,128)} %slot_ref.1, bf16[64,1024]{1,0:T(8,128)(2,1)} %bitcast.14, bf16[64,1024]{1,0:T(8,128)(2,1)} %bitcast.15, bf16[4,64,1024]{2,1,0:T(8,128)(2,1)} %feed_rows.1, ...), custom_call_target="tpu_custom_call" | custom-call | tf_op jit(solution)/shard_map/pallas_call | solution.py:381
  60.9 1.6 %copy.19 = bf16[1,64,1024]{2,1,0:T(8,128)(2,1)} copy(bf16[1,64,1024]{2,1,0:T(8,128)(2,1)} %bitcast.17) | data formatting | bytes 262144
  62.5 1.6 %copy.20 = bf16[1,64,1024]{2,1,0:T(8,128)(2,1)} copy(bf16[1,64,1024]{2,1,0:T(8,128)(2,1)} %bitcast.16) | data formatting | bytes 262144
  64.0 0.0 copy-start
  64.0 3.2 %copy.21 = bf16[1,1024,1024]{2,1,0:T(8,128)(2,1)} copy(bf16[1,1024,1024]{2,1,0:T(8,128)(2,1)} %bitcast.10) | data formatting | bytes 4194304
  67.3 0.0 copy-done
  67.3 0.0 copy-start.1
  67.3 1.3 %copy.22 = bf16[1,1024,1024]{2,1,0:T(8,128)(2,1)} copy(bf16[1,1024,1024]{2,1,0:T(8,128)(2,1)S(1)} %bitcast.9) | data formatting | bytes 4194304
  68.6 0.0 copy-done.1
  68.6 0.6 copy.23
Async XLA Ops:
  64.0 3.2 %copy-start = (bf16[1024,1024]{1,0:T(8,128)(2,1)S(1)}, bf16[1024,1024]{1,0:T(8,128)(2,1)}, u32[]{:S(2)}) copy-start(bf16[1024,1024]{1,0:T(8,128)(2,1)} %get-tuple-element.13) | copy-start | bytes 6291460
  67.3 1.3 %copy-start.1 = (f32[1,1024]{1,0:T(1,128)S(1)}, f32[1,1024]{1,0:T(1,128)}, u32[]{:S(2)}) copy-start(f32[1,1024]{1,0:T(1,128)} %get-tuple-element.24) | copy-start | bytes 12292

commit v2 on v1

--- a/solution.py
+++ b/solution.py
@@ -24,20 +24,24 @@
 def kernel(
     sections,
     peers,
-    slot_ref,
+    slot_hbm,
     arrive_rows,
     arrive_grads,
     feed_rows,
     feed_grads,
-    stashed,
-    win,
-    wout,
-    gain,
+    stash_hbm,
+    win_hbm,
+    wout_hbm,
+    gain_hbm,
     depart_rows,
     depart_grads,
     enter_out,
     leave_out,
     gain_out,
+    stashed,
+    win,
+    wout,
+    gain,
     rows_in,
     grads_in,
     part_send,
@@ -62,6 +66,10 @@
     sum_rsem,
     gain_ssem,
     gain_rsem,
+    load_sem,
+    feed_sem,
+    slot_ref,
+    gain_row,
 ):
     sec = lax.axis_index("section")
     me = lax.axis_index("mp")
@@ -71,14 +79,53 @@
     not_first = sec > 0
     not_last = sec < sections - 1
 
+    pairs = (me, 3 - me, lax.rem(5 - me, 4), lax.rem(me + 2, 4)) if peers == 4 else None
+
     def ahead(k):
-        return lax.rem(me + k, peers)
+        return lax.rem(me + k, peers) if pairs is None else pairs[k]
 
     def behind(k):
-        return lax.rem(me + peers - k, peers)
+        return lax.rem(me + peers - k, peers) if pairs is None else pairs[k]
+
+    order = list(range(1, peers)) + [0]
+    loads = [
+        pltpu.make_async_copy(source, target, load_sem.at[i])
+        for i, (source, target) in enumerate(
+            ((win_hbm, win), (wout_hbm, wout), (stash_hbm, stashed), (gain_hbm, gain_row), (slot_hbm, slot_ref))
+        )
+    ]
+
+    def load(way, t, p):
+        cut = span(p)
+        if isinstance(t, int) and t == 0:
+            source = (arrive_rows, arrive_grads)[way].at[:, cut]
+        else:
+            source = (feed_rows, feed_grads)[way].at[t - 1, :, cut]
+        return pltpu.make_async_copy(
+            source, (rows_in, grads_in)[way].at[t, p], feed_sem.at[way, t, p]
+        )
 
     def span(p):
         return pl.ds(pl.multiple_of(p * block, block), block)
+
+    for p in range(peers):
+        load(0, 0, p).start()
+    for i in (3, 0, 1, 2, 4):
+        loads[i].start()
+    for p in range(peers):
+        load(1, 0, p).start()
+
+    @pl.when(sec == 0)
+    def _():
+        for t in range(1, steps):
+            for p in range(peers):
+                load(0, t, p).start()
+
+    @pl.when(sec == sections - 1)
+    def _():
+        for t in range(1, steps):
+            for p in range(peers):
+                load(1, t, p).start()
 
     barrier = pltpu.get_barrier_semaphore()
 
@@ -103,23 +150,6 @@
         + peers * jnp.where(not_first, 1, 0)
         + peers * jnp.where(not_last, 1, 0)
     )
-
-    for p in range(peers):
-        cut = pl.ds(p * block, block)
-        rows_in[0, p] = arrive_rows[:, cut]
-        grads_in[0, p] = arrive_grads[:, cut]
-
-    @pl.when(sec == 0)
-    def _():
-        for t in range(1, steps):
-            for p in range(peers):
-                rows_in[t, p] = feed_rows[t - 1, :, pl.ds(p * block, block)]
-
-    @pl.when(sec == sections - 1)
-    def _():
-        for t in range(1, steps):
-            for p in range(peers):
-                grads_in[t, p] = feed_grads[t - 1, :, pl.ds(p * block, block)]
 
     gain_acc[...] = jnp.zeros_like(gain_acc)
 
@@ -155,15 +185,26 @@
             device_id_type=MESH,
         ).wait_recv()
 
+    def arrived(way, t, k, travels):
+        @pl.when(t == 0)
+        def _():
+            load(way, 0, behind(k)).wait()
+
+        @pl.when((t > 0) & jnp.logical_not(travels))
+        def _():
+            load(way, t, behind(k)).wait()
+
+        @pl.when((t > 0) & travels)
+        def _():
+            sum_wait(way, t - 1, k)
+
     def forward(t):
         total = jnp.zeros((rows, hidden_width), F32)
         squares = jnp.zeros((rows, 1), F32)
         for k in range(peers):
             p = behind(k)
 
-            @pl.when((t > 0) & not_first)
-            def _():
-                sum_wait(0, t - 1, k)
+            arrived(0, t, k, not_first)
 
             wide = rows_in[t, p].astype(F32)
             scaled = (wide * gain[:, span(p)]).astype(BF16)
@@ -176,8 +217,9 @@
         @pl.when(t == 0)
         def _():
             pl.semaphore_wait(barrier, expected)
-
-        for k in list(range(1, peers)) + [0]:
+            loads[1].wait()
+
+        for k in order:
             part = dot(hidden, wout[:, span(ahead(k))], 1, 0)
             if k:
                 part_send[0, t, k - 1] = part.astype(BF16)
@@ -185,50 +227,41 @@
             else:
                 own_rows[...] = part + rows_in[t, me].astype(F32)
 
-    def prepare():
-        for t in range(steps):
-            slot = stashed[slot_ref[0, t]]
-            slot_rows[t] = slot
-            wide = slot.astype(F32)
-            slot_scaled[t] = (wide * gain[...]).astype(BF16)
-            slot_inverse[t] = lax.rsqrt(
-                jnp.sum(wide * wide, axis=1, keepdims=True) / width + epsilon
-            )
-        flat = slot_scaled[...].reshape(steps * rows, width)
-        slot_proj[...] = dot(flat, win[...], 1, 0).reshape(steps, rows, hidden_width)
-
-        def shape_slot(t, carry):
-            z = slot_inverse[t] * slot_proj[t]
-            inner = ROOT * (z + CUBE * (z * z * z))
-            bend = jnp.tanh(inner)
-            half = 0.5 * z
-            slot_hidden[t] = (half + half * bend).astype(BF16)
-            slot_slope[t] = 0.5 * (1.0 + bend) + half * (1.0 - bend * bend) * (
-                ROOT * (1.0 + (3.0 * CUBE) * (z * z))
-            )
-            return carry
-
-        lax.fori_loop(0, steps, shape_slot, 0)
+    def prepare(t):
+        slot = stashed[slot_ref[0, t]]
+        slot_rows[t] = slot
+        wide = slot.astype(F32)
+        scaled = (wide * gain[...]).astype(BF16)
+        slot_scaled[t] = scaled
+        inverse = lax.rsqrt(jnp.sum(wide * wide, axis=1, keepdims=True) / width + epsilon)
+        slot_inverse[...] = inverse
+        projected = dot(scaled, win[...], 1, 0)
+        slot_proj[...] = projected
+        z = inverse * projected
+        bend = jnp.tanh(ROOT * (z + CUBE * (z * z * z)))
+        half = 0.5 * z
+        slot_hidden[t] = (half + half * bend).astype(BF16)
+        slot_slope[...] = 0.5 * (1.0 + bend) + half * (1.0 - bend * bend) * (
+            ROOT * (1.0 + (3.0 * CUBE) * (z * z))
+        )
 
     def backward(t):
         total = jnp.zeros((rows, hidden_width), F32)
         for k in range(peers):
             p = behind(k)
 
-            @pl.when((t > 0) & not_last)
-            def _():
-                sum_wait(1, t - 1, k)
+            arrived(1, t, k, not_last)
 
             piece = grads_in[t, p]
             grads_all[t, :, span(p)] = piece
             total = total + dot(piece, wout[:, span(p)], 1, 1)
-        pre_grad = total * slot_slope[t]
-        inverse = slot_inverse[t]
+        pre_grad = total * slot_slope[...]
+        inverse = slot_inverse[...]
         update = (inverse * pre_grad).astype(BF16)
         slot_update[t] = update
-        dots = jnp.sum(pre_grad * slot_proj[t], axis=1, keepdims=True)
+        dots = jnp.sum(pre_grad * slot_proj[...], axis=1, keepdims=True)
         factor = -dots * (inverse * inverse * inverse) / width
-        for k in list(range(1, peers)) + [0]:
+        for k in order:
             p = ahead(k)
             raw = dot(update, win[span(p), :], 1, 1)
             wide = slot_rows[t, :, span(p)].astype(F32)
@@ -251,7 +284,7 @@
 
         @pl.when((t < steps - 1) & (not_last if way == 0 else not_first))
         def _():
-            for k in range(peers):
+            for k in order:
                 sum_copy(way, t, k, sec + 1 if way == 0 else sec - 1, ahead(k)).start()
 
         @pl.when(t == steps - 1)
@@ -300,7 +333,10 @@
 
         @pl.when(t == 0)
         def _():
-            prepare()
+            loads[2].wait()
+            loads[4].wait()
+
+        prepare(t)
 
         backward(t)
 
@@ -320,6 +356,9 @@
         reduce(1, t)
         return carry
 
+    loads[3].wait()
+    gain[...] = gain_row[...].astype(F32)
+    loads[0].wait()
     lax.fori_loop(0, steps, step, 0)
     enter_grad()
 
@@ -356,6 +395,15 @@
         return carry
 
     lax.fori_loop(0, steps, drain, 0)
+
+
+def flush(*refs):
+    sems = refs[10]
+    copies = [pltpu.make_async_copy(refs[i], refs[i + 5], sems.at[i]) for i in range(5)]
+    for copy in copies:
+        copy.start()
+    for copy in copies:
+        copy.wait()
 
 
 def solution(mesh):
@@ -377,19 +425,25 @@
         hidden_width = enter_weight.shape[2]
         block = width // peers
         vmem = pl.BlockSpec(memory_space=pltpu.VMEM)
+        hbm = pl.BlockSpec(memory_space=pltpu.HBM)
         dma = pltpu.SemaphoreType.DMA
+        kinds = (
+            ((rows, width), BF16),
+            ((rows, width), BF16),
+            ((width, hidden_width), BF16),
+            ((hidden_width, width), BF16),
+            ((1, width), F32),
+        )
         outs = pl.pallas_call(
             functools.partial(kernel, sections, peers),
-            out_shape=(
-                jax.ShapeDtypeStruct((rows, width), BF16),
-                jax.ShapeDtypeStruct((rows, width), BF16),
-                jax.ShapeDtypeStruct((width, hidden_width), BF16),
-                jax.ShapeDtypeStruct((hidden_width, width), BF16),
-                jax.ShapeDtypeStruct((1, width), F32),
-            ),
-            in_specs=[pl.BlockSpec(memory_space=pltpu.SMEM)] + [vmem] * 8,
+            out_shape=tuple(pltpu.VMEM(shape, kind) for shape, kind in kinds),
+            in_specs=[hbm] * 9,
             out_specs=[vmem] * 5,
             scratch_shapes=[
+                pltpu.VMEM((steps, rows, width), BF16),
+                pltpu.VMEM((width, hidden_width), BF16),
+                pltpu.VMEM((hidden_width, width), BF16),
+                pltpu.VMEM((1, width), F32),
                 pltpu.VMEM((steps + 1, peers, rows, block), BF16),
                 pltpu.VMEM((steps + 1, peers, rows, block), BF16),
                 pltpu.VMEM((2, steps, peers - 1, rows, block), BF16),
@@ -400,9 +454,9 @@
                 pltpu.VMEM((steps, rows, width), BF16),
                 pltpu.VMEM((steps, rows, width), BF16),
                 pltpu.VMEM((steps, rows, hidden_width), BF16),
-                pltpu.VMEM((steps, rows, hidden_width), F32),
-                pltpu.VMEM((steps, rows, hidden_width), F32),
-                pltpu.VMEM((steps, rows, 1), F32),
+                pltpu.VMEM((rows, hidden_width), F32),
+                pltpu.VMEM((rows, hidden_width), F32),
+                pltpu.VMEM((rows, 1), F32),
                 pltpu.VMEM((steps, rows, hidden_width), BF16),
                 pltpu.VMEM((steps, rows, width), BF16),
                 pltpu.VMEM((peers, 8, block), F32),
@@ -414,21 +468,38 @@
                 dma((2, steps, peers)),
                 dma((peers - 1,)),
                 dma((peers - 1,)),
+                dma((5,)),
+                dma((2, steps, peers)),
+                pltpu.SMEM((1, steps), jnp.int32),
+                pltpu.VMEM((1, width), BF16),
             ],
             compiler_params=pltpu.CompilerParams(
-                collective_id=0, has_side_effects=True, vmem_limit_bytes=56 * 1024 * 1024
+                collective_id=0, has_side_effects=True, vmem_limit_bytes=40_000_000
             ),
         )(
-            slot_order,
-            arrive_rows[0],
-            arrive_grads[0],
-            feed_rows,
-            feed_grads,
-            stashed_rows[0],
-            enter_weight[0],
-            leave_weight[0],
-            norm_gain.astype(F32),
-        )
+            *[
+                pltpu.with_memory_space_constraint(block_in, pltpu.HBM)
+                for block_in in (
+                    slot_order,
+                    arrive_rows[0],
+                    arrive_grads[0],
+                    feed_rows,
+                    feed_grads,
+                    stashed_rows[0],
+                    enter_weight[0],
+                    leave_weight[0],
+                    norm_gain,
+                )
+            ],
+        )
+        outs = pl.pallas_call(
+            flush,
+            out_shape=tuple(jax.ShapeDtypeStruct(shape, kind) for shape, kind in kinds),
+            in_specs=[pl.BlockSpec(memory_space=pl.ANY)] * 5,
+            out_specs=[hbm] * 5,
+            scratch_shapes=[dma((5,))],
+            compiler_params=pltpu.CompilerParams(vmem_limit_bytes=1024 * 1024),
+        )(*[pltpu.with_memory_space_constraint(out, pltpu.VMEM) for out in outs])
         rows_out, grads_out, enter_total, leave_total, gain_total = outs
         return (
             rows_out[None],

time: 69.4 us -> 56.7 us (0.82)
  local copies, waits for them, and re-layouts: 8.28 us -> 0 us
  Pallas kernels: 59 us -> 55.9 us
  other arithmetic: 1.28 us -> 0 us
    unnamed x9 -> x0, local copies, waits for them, and re-layouts: 8.28 us -> none
    pallas_call x1 -> x2, Pallas kernels: 59 us -> 55.9 us  [the longest x1 53.8 us: local(): pl.pallas_call(functools.partial(kernel, sections, peers), out_shape=tupl...]
    convert_element_type x1 -> x0, other arithmetic: 1.28 us -> none  [local(): norm_gain.astype(F32)]
where the time goes in v2:
time: 56.7 us; the launch traced here: 56.6 us
  Pallas kernels  55.9 us (99%)
  between operations  0.64 us (1%)
    pallas_call x1, Pallas kernels, local(): pl.pallas_call(functools.partial(kernel, sections, peers), out_shape=tupl...  53.8 us
    pallas_call x1, Pallas kernels, local(): pl.pallas_call(flush, out_shape=tuple((jax.ShapeDtypeStruct(shape, kind)...  2.14 us

profile of v2, /device:TPU:0, one launch (start us, length us, event | category | flops | bytes accessed | tf_op | source)
XLA Modules:
  0.0 56.6 jit_solution(8660791701306783021)
XLA Ops:
  0.6 53.8 %shard_map.128 = (bf16[64,1024]{1,0:T(8,128)(2,1)S(1)}, bf16[64,1024]{1,0:T(8,128)(2,1)S(1)}, bf16[1024,1024]{1,0:T(8,128)(2,1)S(1)}, bf16[1024,1024]{1,0:T(8,128)(2,1)S(1)}, f32[1,1024]{1,0:T(1,128)S(1)}) custom-call(s32[1,5]{1,0:T(1,128)} %slot_hbm.1, bf16[64,1024]{1,0:T(8,128)(2,1)} %bitcast.12, bf16[64,1024]{1,0:T(8,128)(2,1)} %bitcast.13, ...), custom_call_target="tpu_custom_call" | custom-call | tf_op jit(solution)/shard_map/pallas_call | solution.py:437
  54.4 2.1 %shard_map.129 = (bf16[64,1024]{1,0:T(8,128)(2,1)}, bf16[64,1024]{1,0:T(8,128)(2,1)}, bf16[1024,1024]{1,0:T(8,128)(2,1)}, bf16[1024,1024]{1,0:T(8,128)(2,1)}, f32[1,1024]{1,0:T(1,128)}) custom-call(bf16[64,1024]{1,0:T(8,128)(2,1)S(1)} %get-tuple-element.15.refs_0_, bf16[64,1024]{1,0:T(8,128)(2,1)S(1)} %get-tuple-element.16.refs_1_, ...), custom_call_target="tpu_custom_call" | custom-call | tf_op jit(solution)/shard_map/pallas_call | solution.py:495
